TPU v7x, 32 devices: a whole 2x2x4 slice. The times are simulated.
32 devices in a mesh: gx: 8 (over y, x, core), gy: 4 (over z).
Axes of the slice: x: 2, y: 2, z: 4, core: 2. Of those that a mesh axis runs over, the one named last changes fastest.
Arguments:
- products: bfloat16 [1536, 3, 2048], P('gy', None, 'gx'), may hold values from -6 to 6
- operator: bfloat16 [1536, 1536], P(None, 'gy'), may hold values from -0.21875 to 0.21875
Outputs:
- derivative: bfloat16 [1536, 3, 2048], P(('gy', 'gx'))
All inputs are finite; a program needn't handle non-finite values.
Results may differ from a plain program's by a relative error of at most 0.002.
Values may be sent and summed in bfloat16 or wider, within the bound.
A program may use at most 64 MiB of HBM per device.

v0:
```python
import jax
import jax.numpy as jnp
from jax import lax
from jax.sharding import PartitionSpec as P


def body(products, operator):
    y_local, three, m_local = products.shape
    flat = products.reshape(y_local, three * m_local)
    summed = lax.psum_scatter(
        jnp.dot(operator, flat, preferred_element_type=jnp.float32),
        "gy",
        scatter_dimension=0,
        tiled=True,
    )
    result = summed.astype(jnp.bfloat16).reshape(y_local, three, m_local)
    return lax.all_to_all(result, "gx", split_axis=0, concat_axis=2, tiled=True)


def solution(mesh):
    return jax.shard_map(
        body,
        mesh=mesh,
        in_specs=(P("gy", None, "gx"), P(None, "gy")),
        out_specs=P(("gy", "gx"), None, None),
        check_vma=False,
    )
```

profile of v0, /device:TPU:0, one launch (start us, length us, event | category | flops | bytes accessed | tf_op | source)
XLA Modules:
  0.0 125.9 jit_solution(14700882482431408080)
XLA Ops:
  6.5 0.0 copy-start
  6.5 0.0 reduce-scatter.2.cloned.1.call-start
  6.5 1.5 %copy.14 = bf16[384,3,256]{0,2,1:T(8,128)(2,1)S(1)} copy(bf16[384,3,256]{2,0,1:T(8,128)(2,1)} %param.2) | data formatting | bytes 1179648 | tf_op args[0]
  8.0 0.0 copy-done
  8.0 3.5 %fusion = f32[1536,768]{1,0:T(8,128)} fusion(bf16[1536,384]{1,0:T(8,128)(2,1)S(1)} %copy-done, bf16[384,768]{0,1:T(8,128)(2,1)S(1)} %bitcast.9), kind=kOutput, calls=%fused_computation | convolution fusion | flops 905969664 | bytes 6488064 | tf_op jit(solution)/shard_map/dot_general | solution.py:11
  11.5 0.0 reduce-scatter.2.cloned.1.call-update
  11.6 88.2 %reduce-scatter.2.cloned.1.call-done = f32[384,768]{1,0:T(8,128)} async-done(((f32[1536,768]{1,0:T(8,128)}), f32[384,768]{1,0:T(8,128)}) %reduce-scatter.2.cloned.1.call-update) | async-done | bytes 1179664 | tf_op jit(solution)/shard_map/reduce_scatter | solution.py:10
  99.7 1.3 %convert_element_type.3 = bf16[384,768]{1,0:T(8,128)(2,1)S(1)} convert(f32[384,768]{1,0:T(8,128)} %reduce-scatter.2.cloned.1.call-done) | non-fusion elementwise | flops 294912 | bytes 1769472 | tf_op jit(solution)/shard_map/convert_element_type | solution.py:16
  101.1 0.3 copy.15
  101.4 0.8 copy.16
  102.2 16.0 %all_to_all.18 = bf16[384,3,256]{2,1,0:T(4,128)(2,1)S(1)} all-to-all(bf16[384,3,256]{2,1,0:T(4,128)(2,1)S(1)} %copy.16), channel_id=1, replica_groups=mesh['gx'=8,'gy'=4] {'gx'}, dimensions={0} | all-to-all | bytes 1179648 | tf_op jit(solution)/shard_map/all_to_all | solution.py:17
  118.1 0.1 copy.17
  118.2 0.9 copy.19
Async XLA Ops:
  6.5 1.5 %copy-start = (bf16[1536,384]{1,0:T(8,128)(2,1)S(1)}, bf16[1536,384]{1,0:T(8,128)(2,1)}, u32[]{:S(2)}) copy-start(bf16[1536,384]{1,0:T(8,128)(2,1)} %param.3) | copy-start | bytes 3538948
  6.5 93.2 %reduce-scatter.2.cloned.1.call-start = ((), (), s32[]{:S(2)}) async-start(), calls=%async_computation.2 | async-start | bytes 5898240 | tf_op jit(solution)/shard_map/reduce_scatter | solution.py:10
Sparse Core Ops, SparseCore 0:
  11.7 88.0 reduce-scatter.1
where the time goes:
time: 126 us
  waiting for transfers between devices  88.2 us (70%)
  blocking collectives  16 us (13%)
  between operations  13.4 us (11%)
  matrix products  3.53 us (3%)
  local copies, waits for them, and re-layouts  3.49 us (3%)
  other arithmetic  1.33 us (1%)
    reduce_scatter x1, waiting for transfers between devices, body(): lax.psum_scatter(jnp.dot(operator, flat, preferred_element_type=jnp.float...  88.2 us
    all_to_all x1, blocking collectives, body(): return lax.all_to_all(result, 'gx', split_axis=0, concat_axis=2, tiled=True)  16 us
    dot_general x1, matrix products, body(): jnp.dot(operator, flat, preferred_element_type=jnp.float32)  3.53 us
  transfers between devices with their start and end apart: 1, of which 1 were waited for; matrix products, arithmetic and copies ran while one was open for 0% of the time, Pallas kernels for 0%

commit v1 on v0

v1 whole, which is shorter than its diff:
```python
import functools

import jax
import jax.numpy as jnp
from jax import lax
from jax.experimental import pallas as pl
from jax.experimental.pallas import tpu as pltpu
from jax.sharding import PartitionSpec as P

MESH = pl.DeviceIdType.MESH
LANES = 128
SUBLANES = 16
VMEM_BYTES = 60 * 1024 * 1024


def kernel(n, g, parts, p_ref, op_ref, out_ref, blocks, ops, res,
           own_send, fwd_send, op_send, spread_send, res_send, blk_recv, op_recv, out_recv):
    j, k = lax.axis_index("gx"), lax.axis_index("gy")
    half = n // 2
    side = lax.div(k, half)
    step = 1 - 2 * side
    centre = jnp.where(side == 0, half - 1, half)
    other = n - 1 - centre
    is_centre = k == centre
    planes, rows, cols = p_ref.shape
    width = cols // parts
    chunks = planes * parts
    piece = half * rows // g
    outrows = rows // g

    def near(d):
        return centre - step * d

    def far(d):
        return other + step * d

    barrier = pltpu.get_barrier_semaphore()
    greeted = 0
    for dk in range(half):
        kk = side * half + lax.rem(k - side * half + dk, half)
        for dj in range(g):
            if dk or dj:
                pl.semaphore_signal(barrier, inc=1, device_id=(lax.rem(j + dj, g), kk), device_id_type=MESH)
                greeted += 1
    for dk in range(half):
        pl.semaphore_signal(barrier, inc=1, device_id=(j, (1 - side) * half + dk), device_id_type=MESH)
        greeted += 1
    pl.semaphore_wait(barrier, greeted)

    def remote(src, dst, send, recv, gx, gy):
        return pltpu.make_async_remote_copy(
            src_ref=src, dst_ref=dst, send_sem=send, recv_sem=recv,
            device_id=(gx, gy), device_id_type=MESH)

    def wait_bytes(ref, sem):
        pltpu.make_async_copy(ref, ref, sem).wait()

    def chunk_of(ref, i):
        c, h = lax.div(i, parts), lax.rem(i, parts)
        return ref.at[c, :, pl.ds(pl.multiple_of(h * width, width), width)]

    def piece_rows(at):
        return pl.ds(pl.multiple_of(at * piece, piece), piece)

    def op_out(slot, to_side, to):
        at = pl.multiple_of(to_side * (half * rows) + j * piece, piece)
        remote(op_ref.at[pl.ds(at, piece), :], ops.at[k, piece_rows(j), :],
               op_send.at[slot], op_recv.at[k, j], j, to).start()

    def block_out(to):
        for i in range(chunks):
            remote(chunk_of(p_ref, i), chunk_of(blocks.at[k], i), own_send, blk_recv.at[k, i], j, to).start()

    @pl.when(is_centre)
    def _():
        op_out(0, 1 - side, other)
        block_out(other)

        sources = [near(d) for d in range(1, half)] + [far(d) for d in range(half)]
        sibling = j + 1 - 2 * lax.rem(j, 2)

        def spread(s, at, to):
            part = ops.at[s, piece_rows(at), :]
            remote(part, part, spread_send.at[s], op_recv.at[s, at], to, k).start()

        def arrived(s, at):
            part = ops.at[s, piece_rows(at), :]
            wait_bytes(part, op_recv.at[s, at])

        for s in sources:
            arrived(s, j)
            for d in range(1, g // 2):
                spread(s, j, lax.rem(j + 2 * d, g))
            spread(s, j, sibling)
        for s in sources:
            for d in range(1, g // 2):
                at = lax.rem(j + 2 * d, g)
                arrived(s, at)
                spread(s, at, sibling)
        for i in range(chunks):
            for d in range(1, half):
                s = near(d)
                part = chunk_of(blocks.at[s], i)
                wait_bytes(part, blk_recv.at[s, i])
                remote(part, part, fwd_send.at[d - 1], blk_recv.at[s, i], j, other).start()
        for s in sources:
            for d in range(g // 2):
                arrived(s, lax.rem(sibling + 2 * d, g))

        def one(i, carry):
            c, h = lax.div(i, parts), lax.rem(i, parts)
            lane = pl.ds(pl.multiple_of(h * width, width), width)
            for d in range(half):
                part = chunk_of(blocks.at[far(d)], i)
                wait_bytes(part, blk_recv.at[far(d), i])
            target = pl.ds(pl.multiple_of(j * cols + h * width, width), width)
            for d in reversed(range(half)):
                at = pl.multiple_of(near(d) * rows, rows)
                rel = pl.multiple_of((near(d) - side * half) * rows, rows)
                total = jnp.dot(op_ref[pl.ds(at, rows), :], p_ref[c, :, lane], preferred_element_type=jnp.float32)
                for s in sources:
                    total += jnp.dot(ops[s, pl.ds(rel, rows), :], blocks[s, c, :, lane],
                                     preferred_element_type=jnp.float32)
                res[d, c, :, lane] = total.astype(res.dtype)
                for dj in range(1, g) if d == 0 else range(g):
                    to = lax.rem(j + dj, g)
                    remote(res.at[d, c, pl.ds(pl.multiple_of(to * outrows, outrows), outrows), lane],
                           out_ref.at[c, :, target], res_send.at[d], out_recv, to, near(d)).start()
                if d == 0:
                    pltpu.make_async_copy(
                        res.at[d, c, pl.ds(pl.multiple_of(j * outrows, outrows), outrows), lane],
                        out_ref.at[c, :, target], out_recv).start()
            return carry

        lax.fori_loop(0, chunks, one, 0)
        wait_bytes(ops.at[0, piece_rows(0), :], op_send.at[0])
        wait_bytes(p_ref, own_send)
        for d in range(1, half):
            wait_bytes(blocks.at[near(d)], fwd_send.at[d - 1])
        for s in sources:
            for _ in range(1):
                wait_bytes(ops.at[s, pl.ds(0, (g - 1) * piece), :], spread_send.at[s])
        for d in range(half):
            sent = rows - outrows if d == 0 else rows
            wait_bytes(res.at[d, :, pl.ds(0, sent), :], res_send.at[d])

    @pl.when(jnp.logical_not(is_centre))
    def _():
        op_out(0, 1 - side, other)
        op_out(1, side, centre)
        block_out(centre)
        wait_bytes(ops.at[0, piece_rows(0), :], op_send.at[0])
        wait_bytes(ops.at[0, piece_rows(0), :], op_send.at[1])
        wait_bytes(p_ref, own_send)

    wait_bytes(out_ref, out_recv)


def at_centres(n, g, products, operator):
    rows, planes, cols = products.shape
    parts = 2 if cols % (2 * LANES) == 0 else 1
    half = n // 2
    chunks = planes * parts
    out = pl.pallas_call(
        functools.partial(kernel, n, g, parts),
        out_shape=jax.ShapeDtypeStruct((planes, rows // g, cols * g), jnp.bfloat16),
        in_specs=[pl.BlockSpec(memory_space=pltpu.VMEM)] * 2,
        out_specs=pl.BlockSpec(memory_space=pltpu.VMEM),
        scratch_shapes=[
            pltpu.VMEM((n, planes, rows, cols), jnp.bfloat16),
            pltpu.VMEM((n, half * rows, rows), jnp.bfloat16),
            pltpu.VMEM((half, planes, rows, cols), jnp.bfloat16),
            pltpu.SemaphoreType.DMA,
            pltpu.SemaphoreType.DMA((half,)),
            pltpu.SemaphoreType.DMA((2,)),
            pltpu.SemaphoreType.DMA((n,)),
            pltpu.SemaphoreType.DMA((half,)),
            pltpu.SemaphoreType.DMA((n, chunks)),
            pltpu.SemaphoreType.DMA((n, g)),
            pltpu.SemaphoreType.DMA,
        ],
        compiler_params=pltpu.CompilerParams(
            collective_id=0, has_side_effects=True, vmem_limit_bytes=VMEM_BYTES),
    )(products.transpose(1, 0, 2), operator)
    return out.transpose(1, 0, 2)


def by_collectives(products, operator):
    y_local, three, m_local = products.shape
    flat = products.reshape(y_local, three * m_local)
    summed = lax.psum_scatter(
        jnp.dot(operator, flat, preferred_element_type=jnp.float32), "gy", scatter_dimension=0, tiled=True)
    result = summed.astype(jnp.bfloat16).reshape(y_local, three, m_local)
    return lax.all_to_all(result, "gx", split_axis=0, concat_axis=2, tiled=True)


def solution(mesh):
    n, g = mesh.shape["gy"], mesh.shape["gx"]

    def body(products, operator):
        rows, planes, cols = products.shape
        aligned = (n % 2 == 0 and g % 2 == 0 and rows % (g * SUBLANES) == 0
                   and rows % LANES == 0 and cols % LANES == 0)
        held = 2 * (products.size * (n + n // 2 + 2) + operator.size * (1 + n // 2))
        if aligned and held < VMEM_BYTES // 2:
            return at_centres(n, g, products, operator)
        return by_collectives(products, operator)

    return jax.shard_map(
        body,
        mesh=mesh,
        in_specs=(P("gy", None, "gx"), P(None, "gy")),
        out_specs=P(("gy", "gx"), None, None),
        check_vma=False,
    )
```

time: 126 us -> 46.1 us (0.37)
  waiting for transfers between devices: 88.2 us -> 0 us
  Pallas kernels: 0 us -> 44 us
  blocking collectives: 16 us -> 0 us
  between operations: 13.4 us -> 0.01 us
  matrix products: 3.53 us -> 0 us
  local copies, waits for them, and re-layouts: 3.49 us -> 1.93 us
  other arithmetic: 1.33 us -> 0 us
    reduce_scatter x1 -> x0, waiting for transfers between devices: 88.2 us -> none  [body(): lax.psum_scatter(jnp.dot(operator, flat, preferred_element_type=jnp.float...]
    pallas_call x0 -> x1, Pallas kernels: none -> 44 us  [at_centres(): pl.pallas_call(functools.partial(kernel, n, g, parts), out_shape=jax.Shap...]
    all_to_all x1 -> x0, blocking collectives: 16 us -> none  [body(): return lax.all_to_all(result, 'gx', split_axis=0, concat_axis=2, tiled=True)]
    dot_general x1 -> x0, matrix products: 3.53 us -> none  [body(): jnp.dot(operator, flat, preferred_element_type=jnp.float32)]
    convert_element_type x1 -> x0, other arithmetic: 1.33 us -> none  [body(): result = summed.astype(jnp.bfloat16).reshape(y_local, three, m_local)]
  transfers between devices with their start and end apart: 1 -> 0, of which waited for: 1 -> 0; matrix products, arithmetic and copies ran while one was open for 0% -> 0% of each run, Pallas kernels for 0% -> 0%
where the time goes in v1:
time: 46.1 us; the launch traced here: 45.9 us
  Pallas kernels  44 us (95%)
  local copies, waits for them, and re-layouts  1.93 us (4%)
    pallas_call x1, Pallas kernels, at_centres(): pl.pallas_call(functools.partial(kernel, n, g, parts), out_shape=jax.Shap...  44 us
    unnamed x1, local copies, waits for them, and re-layouts  1.93 us

profile of v1, /device:TPU:0, one launch (start us, length us, event | category | flops | bytes accessed | tf_op | source)
XLA Modules:
  0.0 45.9 jit_solution(11474092703026164382)
XLA Ops:
  0.0 44.0 %shard_map.28 = bf16[3,48,2048]{2,1,0:T(8,128)(2,1)} custom-call(bf16[3,384,256]{2,1,0:T(8,128)(2,1)} %bitcast.3, bf16[1536,384]{1,0:T(8,128)(2,1)} %op_ref.1), custom_call_target="tpu_custom_call" | custom-call | tf_op jit(solution)/shard_map/pallas_call | solution.py:164
  44.0 1.9 %copy.4 = bf16[48,3,2048]{2,0,1:T(8,128)(2,1)} copy(bf16[48,3,2048]{2,0,1:T(8,128)(2,1)} %bitcast.2) | data formatting | bytes 1179648

commit v2 on v1

v2 whole, which is shorter than its diff:
```python
import functools

import jax
import jax.numpy as jnp
from jax import lax
from jax.experimental import pallas as pl
from jax.experimental.pallas import tpu as pltpu
from jax.sharding import PartitionSpec as P

MESH = pl.DeviceIdType.MESH
LANES = 128
SUBLANES = 16
VMEM_BYTES = 60 * 1024 * 1024
GRANT = 54500 * 1024


def kernel(n, g, parts, p_ref, op_ref, out_ref, blocks, ops, res,
           own_send, fwd_send, op_send, spread_send, res_send, blk_recv, op_recv, out_recv, own_copy, ready):
    j, k = lax.axis_index("gx"), lax.axis_index("gy")
    half = n // 2
    side = lax.div(k, half)
    step = 1 - 2 * side
    centre = jnp.where(side == 0, half - 1, half)
    other = n - 1 - centre
    is_centre = k == centre
    planes, rows, cols = p_ref.shape
    width = cols // parts
    chunks = planes * parts
    piece = half * rows // g
    outrows = rows // g
    ahead, lead = 2, 2 * chunks // 3

    def flip(mask):
        to = j
        for bit in (1 << b for b in range(mask.bit_length())):
            if mask & bit:
                to = to + bit * (1 - 2 * lax.rem(lax.div(j, bit), 2))
        return to

    def near(d):
        return centre - step * d

    def far(d):
        return other + step * d

    rounds = g.bit_length() - 1
    barrier = pltpu.get_barrier_semaphore()

    def signal(sem, gx, gy):
        pl.semaphore_signal(sem, inc=1, device_id=(gx, gy), device_id_type=MESH)

    for b in range(rounds):
        signal(barrier, flip(1 << b), k)

    @pl.when(is_centre)
    def _():
        signal(barrier, j, other)
        for d in range(1, half):
            signal(barrier, j, near(d))
        pl.semaphore_wait(barrier, rounds + half)

    @pl.when(jnp.logical_not(is_centre))
    def _():
        signal(barrier, j, centre)
        pl.semaphore_wait(barrier, rounds + 1)

    def plane_entered():
        for b in range(rounds):
            signal(ready.at[b], flip(1 << b), k)
            pl.semaphore_wait(ready.at[b], 1)

    def remote(src, dst, send, recv, gx, gy):
        return pltpu.make_async_remote_copy(
            src_ref=src, dst_ref=dst, send_sem=send, recv_sem=recv,
            device_id=(gx, gy), device_id_type=MESH)

    def wait_bytes(ref, sem):
        pltpu.make_async_copy(ref, ref, sem).wait()

    def chunk_of(ref, i):
        c, h = lax.div(i, parts), lax.rem(i, parts)
        return ref.at[c, :, pl.ds(pl.multiple_of(h * width, width), width)]

    def piece_rows(at):
        return pl.ds(pl.multiple_of(at * piece, piece), piece)

    def from_source(s):
        return pl.ds(pl.multiple_of(s * rows, rows), rows)

    def op_part(s, at):
        return ops.at[piece_rows(at), from_source(s)]

    def block_part(s, i):
        c, h = lax.div(i, parts), lax.rem(i, parts)
        return blocks.at[c, from_source(s), pl.ds(pl.multiple_of(h * width, width), width)]

    def op_out(slot, to_side, to):
        at = pl.multiple_of(to_side * (half * rows) + j * piece, piece)
        remote(op_ref.at[pl.ds(at, piece), :], op_part(k, j),
               op_send.at[slot], op_recv.at[k, j], j, to).start()

    def block_out(i, to):
        remote(chunk_of(p_ref, i), block_part(k, i), own_send, blk_recv.at[k, i], j, to).start()

    @pl.when(is_centre)
    def _():
        op_out(0, 1 - side, other)
        for i in range(ahead):
            block_out(i, other)
        for d in range(1, half):
            signal(ready.at[rounds], j, near(d))
        own_rows = pl.ds(pl.multiple_of(side * (half * rows), half * rows), half * rows)
        own_ops = pltpu.make_async_copy(op_ref.at[own_rows, :], ops.at[:, from_source(k)], own_copy.at[0])
        own_ops.start()
        own_blocks = pltpu.make_async_copy(p_ref, blocks.at[:, from_source(k), :], own_copy.at[1])
        own_blocks.start()

        plane_entered()
        pl.semaphore_wait(ready.at[rounds], half - 1)

        sources = [near(d) for d in range(1, half)] + [far(d) for d in range(half)]
        sibling = flip(1)

        def spread(s, at, to):
            part = op_part(s, at)
            remote(part, part, spread_send.at[s], op_recv.at[s, at], to, k).start()

        def arrived(s, at):
            part = op_part(s, at)
            wait_bytes(part, op_recv.at[s, at])

        for s in sources:
            arrived(s, j)
            for d in range(1, g // 2):
                spread(s, j, flip(2 * d))
            spread(s, j, sibling)
        def forward(i):
            for d in range(1, half):
                part = block_part(near(d), i)
                wait_bytes(part, blk_recv.at[near(d), i])
                remote(part, part, fwd_send.at[d - 1], blk_recv.at[near(d), i], j, other).start()

        for i in range(lead):
            forward(i)
            if i + ahead < chunks:
                block_out(i + ahead, other)
        for i in range(lead + ahead, chunks):
            block_out(i, other)
        for s in sources:
            for d in range(1, g // 2):
                at = flip(2 * d)
                arrived(s, at)
                spread(s, at, sibling)
        for s in sources:
            for d in range(g // 2):
                arrived(s, flip(2 * d + 1))
        own_ops.wait()
        own_blocks.wait()

        def one(i, carry):
            c, h = lax.div(i, parts), lax.rem(i, parts)
            lane = pl.ds(pl.multiple_of(h * width, width), width)

            @pl.when(i + lead < chunks)
            def _():
                forward(i + lead)

            for d in range(half):
                wait_bytes(block_part(far(d), i), blk_recv.at[far(d), i])
            target = pl.ds(pl.multiple_of(j * cols + h * width, width), width)
            for d in reversed(range(half)):
                rel = pl.multiple_of((near(d) - side * half) * rows, rows)
                total = jnp.dot(ops[pl.ds(rel, rows), :], blocks[c, :, lane], preferred_element_type=jnp.float32)
                res[d, c, :, lane] = total.astype(res.dtype)
                for mask in reversed(range(1 if d == 0 else 0, g)):
                    to = flip(mask)
                    remote(res.at[d, c, pl.ds(pl.multiple_of(to * outrows, outrows), outrows), lane],
                           out_ref.at[c, :, target], res_send.at[d], out_recv, to, near(d)).start()
                if d == 0:
                    pltpu.make_async_copy(
                        res.at[d, c, pl.ds(pl.multiple_of(j * outrows, outrows), outrows), lane],
                        out_ref.at[c, :, target], out_recv).start()
            return carry

        lax.fori_loop(0, chunks, one, 0)
        wait_bytes(op_part(0, 0), op_send.at[0])
        wait_bytes(blocks.at[:, from_source(0), :], own_send)
        for d in range(1, half):
            wait_bytes(blocks.at[:, from_source(0), :], fwd_send.at[d - 1])
        for s in sources:
            wait_bytes(ops.at[pl.ds(0, (g - 1) * piece), from_source(0)], spread_send.at[s])
        for d in range(half):
            sent = rows - outrows if d == 0 else rows
            wait_bytes(res.at[d, :, pl.ds(0, sent), :], res_send.at[d])

    @pl.when(jnp.logical_not(is_centre))
    def _():
        op_out(1, side, centre)
        block_out(0, centre)
        pl.semaphore_wait(ready.at[rounds], 1)
        op_out(0, 1 - side, other)
        for i in range(1, chunks):
            block_out(i, centre)
        plane_entered()
        signal(ready.at[rounds], j, centre)
        wait_bytes(op_part(0, 0), op_send.at[0])
        wait_bytes(op_part(0, 0), op_send.at[1])
        wait_bytes(blocks.at[:, from_source(0), :], own_send)

    wait_bytes(out_ref, out_recv)


def at_centres(n, g, products, operator):
    rows, planes, cols = products.shape
    parts = 2 if cols % (2 * LANES) == 0 else 1
    half = n // 2
    chunks = planes * parts
    out = pl.pallas_call(
        functools.partial(kernel, n, g, parts),
        out_shape=jax.ShapeDtypeStruct((planes, rows // g, cols * g), jnp.bfloat16),
        in_specs=[pl.BlockSpec(memory_space=pl.ANY)] * 2,
        out_specs=pl.BlockSpec(memory_space=pl.ANY),
        scratch_shapes=[
            pltpu.VMEM((planes, n * rows, cols), jnp.bfloat16),
            pltpu.VMEM((half * rows, n * rows), jnp.bfloat16),
            pltpu.VMEM((half, planes, rows, cols), jnp.bfloat16),
            pltpu.SemaphoreType.DMA,
            pltpu.SemaphoreType.DMA((half,)),
            pltpu.SemaphoreType.DMA((2,)),
            pltpu.SemaphoreType.DMA((n,)),
            pltpu.SemaphoreType.DMA((half,)),
            pltpu.SemaphoreType.DMA((n, chunks)),
            pltpu.SemaphoreType.DMA((n, g)),
            pltpu.SemaphoreType.DMA,
            pltpu.SemaphoreType.DMA((2,)),
            pltpu.SemaphoreType.REGULAR((g.bit_length(),)),
        ],
        compiler_params=pltpu.CompilerParams(
            collective_id=0, has_side_effects=True, vmem_limit_bytes=GRANT),
    )(products.transpose(1, 0, 2), operator)
    return out.transpose(1, 0, 2)


def by_collectives(products, operator):
    y_local, three, m_local = products.shape
    flat = products.reshape(y_local, three * m_local)
    summed = lax.psum_scatter(
        jnp.dot(operator, flat, preferred_element_type=jnp.float32), "gy", scatter_dimension=0, tiled=True)
    result = summed.astype(jnp.bfloat16).reshape(y_local, three, m_local)
    return lax.all_to_all(result, "gx", split_axis=0, concat_axis=2, tiled=True)


def solution(mesh):
    n, g = mesh.shape["gy"], mesh.shape["gx"]

    def body(products, operator):
        rows, planes, cols = products.shape
        aligned = (n % 2 == 0 and g & (g - 1) == 0 and g > 1 and rows % (g * SUBLANES) == 0
                   and rows % LANES == 0 and cols % LANES == 0)
        held = 2 * (products.size * (n + n // 2 + 2) + operator.size * (1 + n // 2))
        if aligned and held < VMEM_BYTES // 2:
            return at_centres(n, g, products, operator)
        return by_collectives(products, operator)

    return jax.shard_map(
        body,
        mesh=mesh,
        in_specs=(P("gy", None, "gx"), P(None, "gy")),
        out_specs=P(("gy", "gx"), None, None),
        check_vma=False,
    )
```

time: 46.1 us -> 41.9 us (0.909)
  Pallas kernels: 44 us -> 40.9 us
  local copies, waits for them, and re-layouts: 1.93 us -> 0.82 us
    pallas_call x1, Pallas kernels: 44 us -> 40.9 us  [at_centres(): pl.pallas_call(functools.partial(kernel, n, g, parts), out_shape=jax.Shap...]
    unnamed x1, local copies, waits for them, and re-layouts: 1.93 us -> 0.82 us
where the time goes in v2:
time: 41.9 us; the launch traced here: 41.8 us
  Pallas kernels  40.9 us (98%)
  local copies, waits for them, and re-layouts  0.82 us (2%)
    pallas_call x1, Pallas kernels, at_centres(): pl.pallas_call(functools.partial(kernel, n, g, parts), out_shape=jax.Shap...  40.9 us

profile of v2, /device:TPU:0, one launch (start us, length us, event | category | flops | bytes accessed | tf_op | source)
XLA Modules:
  0.0 41.8 jit_solution(9605169883439234787)
XLA Ops:
  0.0 40.9 %shard_map.28 = bf16[3,48,2048]{2,1,0:T(8,128)(2,1)S(1)} custom-call(bf16[3,384,256]{2,1,0:T(8,128)(2,1)} %bitcast.3, bf16[1536,384]{1,0:T(8,128)(2,1)} %op_ref.1), custom_call_target="tpu_custom_call" | custom-call | tf_op jit(solution)/shard_map/pallas_call | solution.py:218
  41.0 0.8 %copy.4 = bf16[48,3,2048]{2,0,1:T(8,128)(2,1)} copy(bf16[48,3,2048]{2,0,1:T(8,128)(2,1)S(1)} %bitcast.2) | data formatting | bytes 1179648

commit v3 on v2

--- a/solution.py
+++ b/solution.py
@@ -15,7 +15,7 @@
 
 
 def kernel(n, g, parts, p_ref, op_ref, out_ref, blocks, ops, res,
-           own_send, fwd_send, op_send, spread_send, res_send, blk_recv, op_recv, out_recv, own_copy, ready):
+           own_send, fwd_send, op_send, spread_send, res_send, blk_recv, op_recv, out_recv, own_copy, ready, ahead_of):
     j, k = lax.axis_index("gx"), lax.axis_index("gy")
     half = n // 2
     side = lax.div(k, half)
@@ -28,7 +28,7 @@
     chunks = planes * parts
     piece = half * rows // g
     outrows = rows // g
-    ahead, lead = 2, 2 * chunks // 3
+    ahead, lead = 2, chunks - 1
 
     def flip(mask):
         to = j
@@ -142,10 +142,9 @@
 
         for i in range(lead):
             forward(i)
-            if i + ahead < chunks:
+            if i + ahead < lead:
                 block_out(i + ahead, other)
-        for i in range(lead + ahead, chunks):
-            block_out(i, other)
+        block_out(lead, other)
         for s in sources:
             for d in range(1, g // 2):
                 at = flip(2 * d)
@@ -165,12 +164,18 @@
             def _():
                 forward(i + lead)
 
-            for d in range(half):
+            last = far(half - 1)
+            others = pl.ds(pl.multiple_of(side * rows, rows), (n - 1) * rows)
+            for d in range(half - 1):
                 wait_bytes(block_part(far(d), i), blk_recv.at[far(d), i])
+            ahead_of[...] = jnp.dot(ops[:, others], blocks[c, others, lane], preferred_element_type=jnp.float32)
+            wait_bytes(block_part(last, i), blk_recv.at[last, i])
             target = pl.ds(pl.multiple_of(j * cols + h * width, width), width)
             for d in reversed(range(half)):
                 rel = pl.multiple_of((near(d) - side * half) * rows, rows)
-                total = jnp.dot(ops[pl.ds(rel, rows), :], blocks[c, :, lane], preferred_element_type=jnp.float32)
+                total = ahead_of[pl.ds(rel, rows), :] + jnp.dot(
+                    ops[pl.ds(rel, rows), from_source(last)], blocks[c, from_source(last), lane],
+                    preferred_element_type=jnp.float32)
                 res[d, c, :, lane] = total.astype(res.dtype)
                 for mask in reversed(range(1 if d == 0 else 0, g)):
                     to = flip(mask)
@@ -234,6 +239,7 @@
             pltpu.SemaphoreType.DMA,
             pltpu.SemaphoreType.DMA((2,)),
             pltpu.SemaphoreType.REGULAR((g.bit_length(),)),
+            pltpu.VMEM((half * rows, cols // parts), jnp.float32),
         ],
         compiler_params=pltpu.CompilerParams(
             collective_id=0, has_side_effects=True, vmem_limit_bytes=GRANT),
@@ -255,7 +261,7 @@
 
     def body(products, operator):
         rows, planes, cols = products.shape
-        aligned = (n % 2 == 0 and g & (g - 1) == 0 and g > 1 and rows % (g * SUBLANES) == 0
+        aligned = (n % 2 == 0 and planes > 2 and g & (g - 1) == 0 and g > 1 and rows % (g * SUBLANES) == 0
                    and rows % LANES == 0 and cols % LANES == 0)
         held = 2 * (products.size * (n + n // 2 + 2) + operator.size * (1 + n // 2))
         if aligned and held < VMEM_BYTES // 2:

time: 41.9 us -> 40.8 us (0.974)
  Pallas kernels: 40.9 us -> 39.9 us
    pallas_call x1, Pallas kernels: 40.9 us -> 39.9 us  [at_centres(): pl.pallas_call(functools.partial(kernel, n, g, parts), out_shape=jax.Shap...]
where the time goes in v3:
time: 40.8 us; the launch traced here: 40.7 us
  Pallas kernels  39.9 us (98%)
  local copies, waits for them, and re-layouts  0.82 us (2%)
    pallas_call x1, Pallas kernels, at_centres(): pl.pallas_call(functools.partial(kernel, n, g, parts), out_shape=jax.Shap...  39.9 us
    unnamed x1, local copies, waits for them, and re-layouts  0.82 us

profile of v3, /device:TPU:0, one launch (start us, length us, event | category | flops | bytes accessed | tf_op | source)
XLA Modules:
  0.0 40.7 jit_solution(11929372791022864675)
XLA Ops:
  0.0 39.9 %shard_map.28 = bf16[3,48,2048]{2,1,0:T(8,128)(2,1)S(1)} custom-call(bf16[3,384,256]{2,1,0:T(8,128)(2,1)} %bitcast.3, bf16[1536,384]{1,0:T(8,128)(2,1)} %op_ref.1), custom_call_target="tpu_custom_call" | custom-call | tf_op jit(solution)/shard_map/pallas_call | solution.py:223
  39.9 0.8 %copy.4 = bf16[48,3,2048]{2,0,1:T(8,128)(2,1)} copy(bf16[48,3,2048]{2,0,1:T(8,128)(2,1)S(1)} %bitcast.2) | data formatting | bytes 1179648
